TPU v7x, 128 devices: a whole 4x4x4 slice. The times are simulated.
128 devices in a mesh: dp: 32 (over x, z, core), tensor: 4 (over y).
Axes of the slice: x: 4, y: 4, z: 4, core: 2. Of those that a mesh axis runs over, the one named last changes fastest.
Arguments:
- tokens: bfloat16 [2, 2048, 4096], P(None, 'dp', 'tensor'), may hold values from -6 to 6
- routes: int32 [2, 2048, 2], P(None, 'dp'), may hold values from 0 to 7, all different within a row; in each aligned block of 64 rows (0 to 63, 64 to 127, ..., all dimensions but the last counted through in order) at most 20 rows name the same one
- probs: float32 [2, 2048, 8], P(None, 'dp'), may hold values from 0 to 1, as said below
- w_gate: bfloat16 [32, 4096, 3584], P('dp', None, 'tensor'), may hold values from -0.09375 to 0.09375
- w_up: bfloat16 [32, 4096, 3584], P('dp', None, 'tensor'), may hold values from -0.09375 to 0.09375
- w_down: bfloat16 [32, 3584, 4096], P('dp', 'tensor'), may hold values from -0.046875 to 0.046875
Outputs:
- mixed: bfloat16 [2, 2048, 4096], P(None, 'dp', 'tensor')
- aux_loss: float32 [2, 8], replicated
Inputs may be any that keep to these rules, and one draw needn't show every extreme that they name: `routes`: in each aligned block of 64 rows (the rows of one index of dp in one micro-batch) no expert is named in more than 20 entries; the 2 experts of a row differ. `probs`: each row is positive and sums to one.
All inputs are finite; a program needn't handle non-finite values.
Results may differ from a plain program's by a relative error of at most 0.012.
Values may be sent and summed in bfloat16 or wider, within the bound.
A program may use at most 128 MiB of HBM per device.

v0:
```python
import jax
import jax.numpy as jnp
from jax import lax
from jax.sharding import PartitionSpec as P

MICRO = 2
CAP = 20


def together(arrays, axis):
    ravelled, at, gathered = (jnp.concatenate([a.reshape(-1) for a in arrays]), 0, [])
    subtotal = lax.psum(ravelled, axis)
    for a in arrays:
        gathered.append(subtotal[at : at + a.size].reshape(a.shape))
        at += a.size
    return tuple(gathered)


def slot_tables(route, prob):
    rows_count = route.shape[0]
    experts = prob.shape[-1]
    capacity = CAP
    flat = route.reshape(-1)
    onehot = (flat[:, None] == jnp.arange(experts, dtype=jnp.int32)[None, :]).astype(jnp.int32)
    before = jnp.cumsum(onehot, axis=0) - onehot
    place = jnp.sum(before * onehot, axis=1)
    slot = flat * capacity + place
    picked = jnp.take_along_axis(prob, route, axis=1)
    weights = picked / jnp.sum(picked, axis=1, keepdims=True)
    grid = (slot[:, None] == jnp.arange(experts * capacity, dtype=jnp.int32)[None, :]).astype(
        jnp.float32
    )
    grid = grid.reshape(rows_count, route.shape[1], experts * capacity)
    dispatch = jnp.sum(grid, axis=1).T.astype(jnp.bfloat16)
    combine = jnp.sum(grid * weights[:, :, None], axis=1)
    counts = jnp.sum(onehot, axis=0).astype(jnp.float32)
    return (dispatch, combine, counts)


def spread_slots(slots, experts, copies_per, capacity):
    width = slots.shape[-1]
    wide = jnp.broadcast_to(
        slots.reshape(experts, 1, capacity, width), (experts, copies_per, capacity, width)
    )
    return wide.reshape(experts * copies_per, capacity, width)


def local(tokens, routes, probs, w_gate, w_up, w_down):
    groups = lax.axis_size("dp")
    experts = probs.shape[-1]
    copies_per = groups // experts
    capacity = CAP
    gate_local = w_gate[0]
    up_local = w_up[0]
    down_local = w_down[0]
    rows_local = tokens.shape[1]
    total_rows = rows_local * groups
    top_count = routes.shape[-1]
    tables = [slot_tables(routes[index], probs[index]) for index in range(MICRO)]
    prob_local = [jnp.sum(probs[index], axis=0) for index in range(MICRO)]
    count_table, prob_table = together(
        (jnp.stack([tables[index][2] for index in range(MICRO)]), jnp.stack(prob_local)), "dp"
    )
    outputs = []
    loss_terms = []
    for micro_index in range(MICRO):
        dispatch, combine, counts = tables[micro_index]
        count_all = count_table[micro_index]
        prob_all = prob_table[micro_index]
        width_local = tokens.shape[2]
        slots = jnp.dot(dispatch, tokens[micro_index], preferred_element_type=jnp.float32).astype(
            jnp.bfloat16
        )
        arrived = lax.all_to_all(
            spread_slots(slots, experts, copies_per, capacity),
            "dp",
            split_axis=0,
            concat_axis=0,
            tiled=True,
        )
        piece = lax.all_gather(arrived, "tensor", axis=2, tiled=True)
        piece_rows = piece.reshape(-1, piece.shape[2])
        gate = jnp.dot(piece_rows, gate_local, preferred_element_type=jnp.float32)
        up = jnp.dot(piece_rows, up_local, preferred_element_type=jnp.float32)
        hidden = (jax.nn.silu(gate) * up).astype(jnp.bfloat16)
        part = jnp.dot(hidden, down_local, preferred_element_type=jnp.float32).astype(jnp.bfloat16)
        reduced = lax.psum_scatter(part, "tensor", scatter_dimension=1, tiled=True).astype(
            jnp.float32
        )
        returned = lax.all_to_all(
            reduced.reshape(groups, capacity, width_local).astype(jnp.bfloat16),
            "dp",
            split_axis=0,
            concat_axis=0,
            tiled=True,
        ).astype(jnp.float32)
        summed = jnp.sum(returned.reshape(experts, copies_per, capacity, width_local), axis=1)
        mixed = jnp.dot(
            combine,
            summed.reshape(experts * capacity, width_local),
            precision=lax.Precision.HIGHEST,
            preferred_element_type=jnp.float32,
        )
        outputs.append(mixed.astype(jnp.bfloat16))
        loss_terms.append(
            experts * (count_all / (total_rows * top_count)) * (prob_all / total_rows)
        )
    return (jnp.stack(outputs), jnp.stack(loss_terms))


def solution(mesh):
    in_specs = (
        P(None, "dp", "tensor"),
        P(None, "dp", None),
        P(None, "dp", None),
        P("dp", None, "tensor"),
        P("dp", None, "tensor"),
        P("dp", "tensor", None),
    )
    out_specs = (P(None, "dp", "tensor"), P())
    return jax.shard_map(local, mesh=mesh, in_specs=in_specs, out_specs=out_specs, check_vma=False)
```

profile of v0, /device:TPU:1, one launch (start us, length us, event | category | flops | bytes accessed | tf_op | source)
XLA Modules:
  0.0 393.9 jit_solution(13326397115779215763)
XLA Ops:
  7.2 0.7 fusion.46
  7.9 0.7 bitcast_or_fusion.1
  8.6 0.1 copy.32
  8.7 0.1 eq.58
  8.8 0.1 fusion.35
  8.9 0.2 reduce_window_sum.17
  9.1 0.2 fusion.36
  9.3 0.1 reduce_sum.131
  9.4 0.1 copy.33
  9.5 0.1 copy.36
  9.6 0.2 eq.65
  9.8 0.1 fusion.34
  9.9 0.2 reduce_window_sum.18
  10.0 0.2 fusion.37
  10.2 0.1 reduce_sum.137
  10.4 0.1 copy.37
  10.4 0.9 slice_reduce_fusion.1
  11.3 0.1 copy.34
  11.4 0.1 reshape.174
  11.5 1.0 gather_fusion
  12.6 0.1 reshape.177
  12.7 0.1 copy.35
  12.8 0.1 copy.38
  12.9 0.2 reshape.179
  13.0 1.0 gather_fusion.1
  14.1 0.1 reshape.182
  14.2 0.1 copy.39
  14.3 0.1 convert_reduce_fusion.2
  14.5 0.3 convolution_convert_fusion
  14.8 0.1 broadcast_in_dim.13
  14.8 0.2 broadcast_in_dim.14
  15.0 32.2 %all_to_all.20 = bf16[32,20,1024]{2,1,0:T(8,128)(2,1)} all-to-all(bf16[32,20,1024]{2,1,0:T(8,128)(2,1)S(1)} %bitcast.97), channel_id=1, replica_groups=mesh['dp'=32,'tensor'=4] {'dp'}, dimensions={0} | all-to-all | bytes 2621440 | tf_op jit(solution)/shard_map/all_to_all | solution.py:74
  47.3 0.3 convolution_convert_fusion.1
  47.5 0.1 broadcast_in_dim.11
  47.6 0.2 broadcast_in_dim.12
  47.8 26.4 %all_to_all.21 = bf16[32,20,1024]{2,1,0:T(8,128)(2,1)} all-to-all(bf16[32,20,1024]{2,1,0:T(8,128)(2,1)S(1)} %bitcast.98), channel_id=1, replica_groups=mesh['dp'=32,'tensor'=4] {'dp'}, dimensions={0} | all-to-all | bytes 2621440 | tf_op jit(solution)/shard_map/all_to_all | solution.py:74
  74.2 36.0 %all-gather.5.cloned.1.call-done = bf16[32,20,4096]{2,1,0:T(8,128)(2,1)} async-done(((bf16[32,20,1024]{2,1,0:T(8,128)(2,1)}), bf16[32,20,4096]{2,1,0:T(8,128)(2,1)}) %all-gather.5.cloned.1.call-update) | async-done | bytes 5242896 | tf_op jit(solution)/shard_map/all_gather | solution.py:81
  110.3 7.8 %reshape.140 = bf16[640,4096]{1,0:T(8,128)(2,1)} reshape(bf16[32,20,4096]{2,1,0:T(8,128)(2,1)} %all-gather.5.cloned.1.call-done) | data formatting | bytes 10485760 | tf_op jit(solution)/shard_map/reshape | solution.py:82
  118.0 11.7 %fusion.8 = f32[640,896]{1,0:T(8,128)S(1)} fusion(bf16[640,4096]{1,0:T(8,128)(2,1)} %reshape.140, bf16[1,4096,896]{2,1,0:T(8,128)(2,1)} %param.11), kind=kOutput, calls=%fused_computation.10 | convolution fusion | flops 4697620480 | bytes 14876672 | tf_op jit(solution)/shard_map/dot_general | solution.py:83
  129.7 18.9 %fusion.15 = bf16[640,4096]{1,0:T(8,128)(2,1)} fusion(bf16[1,896,4096]{2,1,0:T(8,128)(2,1)} %param.13, f32[640,896]{1,0:T(8,128)S(1)} %fusion.8, bf16[640,4096]{1,0:T(8,128)(2,1)} %reshape.140, bf16[1,4096,896]{2,1,0:T(8,128)(2,1)} %param.12), kind=kOutput, calls=%fused_computation.15 | convolution fusion | flops 9401303040 | bytes 27459584 | tf_op jit(solution)/shard_map/dot_general | solution.py:86
  148.6 0.2 reduce-scatter.3.cloned.1.call-start
  148.8 29.4 %all-gather.3.cloned.1.call-done = bf16[32,20,4096]{2,1,0:T(8,128)(2,1)} async-done(((bf16[32,20,1024]{2,1,0:T(8,128)(2,1)}), bf16[32,20,4096]{2,1,0:T(8,128)(2,1)}) %all-gather.3.cloned.1.call-update) | async-done | bytes 5242896 | tf_op jit(solution)/shard_map/all_gather | solution.py:81
  178.2 7.7 %reshape.135 = bf16[640,4096]{1,0:T(8,128)(2,1)} reshape(bf16[32,20,4096]{2,1,0:T(8,128)(2,1)} %all-gather.3.cloned.1.call-done) | data formatting | bytes 10485760 | tf_op jit(solution)/shard_map/reshape | solution.py:82
  185.9 11.6 %fusion.10 = f32[640,896]{1,0:T(8,128)S(1)} fusion(bf16[640,4096]{1,0:T(8,128)(2,1)} %reshape.135, bf16[1,4096,896]{2,1,0:T(8,128)(2,1)} %param.11), kind=kOutput, calls=%fused_computation.12 | convolution fusion | flops 4697620480 | bytes 14876672 | tf_op jit(solution)/shard_map/dot_general | solution.py:83
  197.5 18.9 %fusion.12 = bf16[640,4096]{1,0:T(8,128)(2,1)} fusion(bf16[1,896,4096]{2,1,0:T(8,128)(2,1)} %param.13, f32[640,896]{1,0:T(8,128)S(1)} %fusion.10, bf16[640,4096]{1,0:T(8,128)(2,1)} %reshape.135, bf16[1,4096,896]{2,1,0:T(8,128)(2,1)} %param.12), kind=kOutput, calls=%fused_computation.14 | convolution fusion | flops 9401303040 | bytes 27459584 | tf_op jit(solution)/shard_map/dot_general | solution.py:86
  216.4 20.4 %reduce-scatter.5.cloned.1.call-done = bf16[640,1024]{1,0:T(8,128)(2,1)} async-done(((bf16[640,4096]{1,0:T(8,128)(2,1)}), bf16[640,1024]{1,0:T(8,128)(2,1)}) %reduce-scatter.5.cloned.1.call-update) | async-done | bytes 1310736 | tf_op jit(solution)/shard_map/reduce_scatter | solution.py:87
  236.8 3.2 convert_element_type.98
  240.0 7.7 %all-to-all-start.3 = ((bf16[32,20,1024]{2,1,0:T(8,128)(2,1)}), bf16[32,20,1024]{2,1,0:T(8,128)(2,1)S(1)}, u32[]{:S(2)}, u32[]{:S(2)}) async-start(bf16[32,20,1024]{2,1,0:T(8,128)(2,1)} %convert_element_type.98), calls=%async_computation.5 | async-start | bytes 3145728 | tf_op jit(solution)/shard_map/all_to_all | solution.py:90
  247.7 46.5 %reduce-scatter.3.cloned.1.call-done = bf16[640,1024]{1,0:T(8,128)(2,1)} async-done(((bf16[640,4096]{1,0:T(8,128)(2,1)}), bf16[640,1024]{1,0:T(8,128)(2,1)}) %reduce-scatter.3.cloned.1.call-update) | async-done | bytes 1310736 | tf_op jit(solution)/shard_map/reduce_scatter | solution.py:87
  294.3 3.2 convert_element_type.90
  297.5 7.7 %all-to-all-start.1 = ((bf16[32,20,1024]{2,1,0:T(8,128)(2,1)}), bf16[32,20,1024]{2,1,0:T(8,128)(2,1)S(1)}, u32[]{:S(2)}, u32[]{:S(2)}) async-start(bf16[32,20,1024]{2,1,0:T(8,128)(2,1)} %convert_element_type.90), calls=%async_computation.2 | async-start | bytes 3145728 | tf_op jit(solution)/shard_map/all_to_all | solution.py:90
  305.2 0.1 reshape.145
  305.3 0.1 reshape.144
  305.4 0.1 pad_maximum_fusion.4
  305.5 76.7 %psum.7 = f32[32]{0:T(128)S(1)} all-reduce(f32[32]{0:T(128)S(1)} %pad_maximum_fusion.4), channel_id=1, replica_groups=mesh['dp'=32,'tensor'=4] {'dp'}, use_global_device_ids=true, to_apply=%region_18.20 | all-reduce | flops 32 | bytes 256 | tf_op jit(solution)/shard_map/psum | solution.py:12
  382.2 0.1 multiply_bitcast_fusion.1
  382.3 0.6 pad_maximum_fusion.3
  382.9 1.2 convert_reduce_fusion
  384.0 1.2 reshape.143
  385.2 0.3 convert_reduce_fusion.1
  385.5 0.1 reshape.138
  385.6 0.5 fusion.29
  386.1 0.5 fusion.28
  386.6 0.7 pad_maximum_fusion
  (20 shorter events, 0.3 us)
Async XLA Ops:
  7.2 103.1 %all-gather.5.cloned.1.call-start = ((), (), s32[]{:S(2)}) async-start(), calls=%async_computation.8 | async-start | bytes 7864320 | tf_op jit(solution)/shard_map/all_gather | solution.py:81
  13.0 1.3 copy-start.1
  13.0 1.5 copy-start
  47.2 131.0 %all-gather.3.cloned.1.call-start = ((), (), s32[]{:S(2)}) async-start(), calls=%async_computation.6 | async-start | bytes 7864320 | tf_op jit(solution)/shard_map/all_gather | solution.py:81
  74.2 162.6 %reduce-scatter.5.cloned.1.call-start = ((), (), s32[]{:S(2)}) async-start(), calls=%async_computation.9 | async-start | bytes 6553600 | tf_op jit(solution)/shard_map/reduce_scatter | solution.py:87
  148.6 145.7 %reduce-scatter.3.cloned.1.call-start = ((), (), s32[]{:S(2)}) async-start(), calls=%async_computation.7 | async-start | bytes 6553600 | tf_op jit(solution)/shard_map/reduce_scatter | solution.py:87
  240.0 57.5 %all-to-all-start.3 = ((bf16[32,20,1024]{2,1,0:T(8,128)(2,1)}), bf16[32,20,1024]{2,1,0:T(8,128)(2,1)S(1)}, u32[]{:S(2)}, u32[]{:S(2)}) async-start(bf16[32,20,1024]{2,1,0:T(8,128)(2,1)} %convert_element_type.98), calls=%async_computation.5 | async-start | bytes 3145728 | tf_op jit(solution)/shard_map/all_to_all | solution.py:90
  297.5 87.7 %all-to-all-start.1 = ((bf16[32,20,1024]{2,1,0:T(8,128)(2,1)}), bf16[32,20,1024]{2,1,0:T(8,128)(2,1)S(1)}, u32[]{:S(2)}, u32[]{:S(2)}) async-start(bf16[32,20,1024]{2,1,0:T(8,128)(2,1)} %convert_element_type.90), calls=%async_computation.2 | async-start | bytes 3145728 | tf_op jit(solution)/shard_map/all_to_all | solution.py:90
Sparse Core Ops, SparseCore 0:
  47.3 62.8 all-gather.4
  111.9 66.2 all-gather.2
  180.6 56.1 reduce-scatter.4
  239.1 55.1 reduce-scatter.2
where the time goes:
time: 395 us; the launch traced here: 394 us
  blocking collectives  135 us (34%)
  waiting for transfers between devices  132 us (33%)
  matrix products  62.5 us (16%)
  local copies, waits for them, and re-layouts  28.3 us (7%)
  starting transfers between devices  15.8 us (4%)
  between operations  14 us (4%)
  other arithmetic  5.56 us (1%)
    psum x1, blocking collectives, together(): subtotal = lax.psum(ravelled, axis)  76.7 us
    reduce_scatter x2, waiting for transfers between devices, local(): lax.psum_scatter(part, 'tensor', scatter_dimension=1, tiled=True)  67 us
    all_gather x2, waiting for transfers between devices, local(): piece = lax.all_gather(arrived, 'tensor', axis=2, tiled=True)  65.4 us
    all_to_all x2, blocking collectives, local(): lax.all_to_all(spread_slots(slots, experts, copies_per, capacity), 'dp',...  58.5 us
    dot_general x2, matrix products, local(): jnp.dot(hidden, down_local, preferred_element_type=jnp.float32)  37.8 us
    dot_general x2, matrix products, local(): gate = jnp.dot(piece_rows, gate_local, preferred_element_type=jnp.float32)  23.2 us
    all_to_all x2, starting transfers between devices, local(): lax.all_to_all(reduced.reshape(groups, capacity, width_local).astype(jnp....  15.4 us
    reshape x2, local copies, waits for them, and re-layouts, local(): piece_rows = piece.reshape(-1, piece.shape[2])  15.4 us
  transfers between devices with their start and end apart: 6, of which 4 were waited for; matrix products, arithmetic and copies ran while one was open for 22% of the time, Pallas kernels for 0%

commit v1 on v0

--- a/solution.py
+++ b/solution.py
@@ -78,7 +78,16 @@
             concat_axis=0,
             tiled=True,
         )
-        piece = lax.all_gather(arrived, "tensor", axis=2, tiled=True)
+        ring = [arrived]
+        for hop in range(3):
+            ring.append(
+                lax.ppermute(ring[-1], "tensor", [(dev, (dev + 1) % 4) for dev in range(4)])
+            )
+        piece = jnp.roll(
+            jnp.concatenate(ring[::-1], axis=2),
+            (lax.axis_index("tensor") + 1) * ring[0].shape[2],
+            axis=2,
+        )
         piece_rows = piece.reshape(-1, piece.shape[2])
         gate = jnp.dot(piece_rows, gate_local, preferred_element_type=jnp.float32)
         up = jnp.dot(piece_rows, up_local, preferred_element_type=jnp.float32)

time: 395 us -> 478 us (1.21)
  waiting for transfers between devices: 132 us -> 175 us
  other arithmetic: 5.56 us -> 29.6 us
  local copies, waits for them, and re-layouts: 28.3 us -> 42 us
    ppermute x0 -> x6, waiting for transfers between devices: none -> 134 us  [local(): lax.ppermute(ring[-1], 'tensor', [(dev, (dev + 1) % 4) for dev in range(4)])]
    all_gather x2 -> x0, waiting for transfers between devices: 65.4 us -> none  [local(): piece = lax.all_gather(arrived, 'tensor', axis=2, tiled=True)]
    reduce_scatter x2, waiting for transfers between devices: 67 us -> 41.4 us  [local(): lax.psum_scatter(part, 'tensor', scatter_dimension=1, tiled=True)]
    concatenate x0 -> x2, other arithmetic: none -> 24 us  [local(): jnp.roll(jnp.concatenate(ring[::-1], axis=2), (lax.axis_index('tensor') +...]
    ppermute x0 -> x6, local copies, waits for them, and re-layouts: none -> 11 us  [local(): lax.ppermute(ring[-1], 'tensor', [(dev, (dev + 1) % 4) for dev in range(4)])]
  transfers between devices with their start and end apart: 6 -> 10, of which waited for: 4 -> 6; matrix products, arithmetic and copies ran while one was open for 22% -> 26% of each run, Pallas kernels for 0% -> 0%
where the time goes in v1:
time: 478 us; the launch traced here: 477 us
  waiting for transfers between devices  175 us (37%)
  blocking collectives  136 us (28%)
  matrix products  61.7 us (13%)
  local copies, waits for them, and re-layouts  42 us (9%)
  other arithmetic  29.6 us (6%)
  starting transfers between devices  18.6 us (4%)
  between operations  14.4 us (3%)
    ppermute x6, waiting for transfers between devices, local(): lax.ppermute(ring[-1], 'tensor', [(dev, (dev + 1) % 4) for dev in range(4)])  134 us
    psum x1, blocking collectives, together(): subtotal = lax.psum(ravelled, axis)  76.7 us
    all_to_all x2, blocking collectives, local(): lax.all_to_all(spread_slots(slots, experts, copies_per, capacity), 'dp',...  58.9 us
    reduce_scatter x2, waiting for transfers between devices, local(): lax.psum_scatter(part, 'tensor', scatter_dimension=1, tiled=True)  41.4 us
    dot_general x2, matrix products, local(): jnp.dot(hidden, down_local, preferred_element_type=jnp.float32)  37.8 us
    concatenate x2, other arithmetic, local(): jnp.roll(jnp.concatenate(ring[::-1], axis=2), (lax.axis_index('tensor') +...  24 us
    dot_general x2, matrix products, local(): gate = jnp.dot(piece_rows, gate_local, preferred_element_type=jnp.float32)  22.4 us
    reshape x2, local copies, waits for them, and re-layouts, local(): piece_rows = piece.reshape(-1, piece.shape[2])  15.6 us
  transfers between devices with their start and end apart: 10, of which 6 were waited for; matrix products, arithmetic and copies ran while one was open for 26% of the time, Pallas kernels for 0%

profile of v1, /device:TPU:1, one launch (start us, length us, event | category | flops | bytes accessed | tf_op | source)
XLA Modules:
  0.0 477.3 jit_solution(12313451920789929633)
XLA Ops:
  7.2 0.7 fusion.60
  7.9 0.7 bitcast_or_fusion.1
  8.6 0.1 copy.68
  8.7 0.1 eq.60
  8.9 0.2 reduce_window_sum.17
  9.1 0.2 fusion.50
  9.3 0.1 reduce_sum.131
  9.6 0.2 eq.67
  9.9 0.2 reduce_window_sum.18
  10.0 0.2 fusion.51
  10.2 0.1 reduce_sum.137
  10.4 0.9 slice_reduce_fusion.1
  11.3 0.1 copy.70
  11.4 0.1 reshape.174
  11.5 1.0 gather_fusion
  12.6 0.1 reshape.177
  12.9 0.2 reshape.179
  13.0 1.0 gather_fusion.1
  14.1 0.1 reshape.182
  14.3 0.1 convert_reduce_fusion.2
  14.5 0.3 convolution_convert_fusion
  14.8 0.2 broadcast_in_dim.14
  15.0 32.0 %all_to_all.20 = bf16[32,20,1024]{2,1,0:T(8,128)(2,1)S(1)} all-to-all(bf16[32,20,1024]{2,1,0:T(8,128)(2,1)S(1)} %bitcast.97), channel_id=1, replica_groups=mesh['dp'=32,'tensor'=4] {'dp'}, dimensions={0} | all-to-all | bytes 2621440 | tf_op jit(solution)/shard_map/all_to_all | solution.py:74
  47.1 0.7 copy.80
  47.8 1.4 collective-permute-start.3
  49.2 30.7 %collective-permute-done.3 = bf16[32,20,1024]{2,0,1:T(8,128)(2,1)} collective-permute-done((bf16[32,20,1024]{2,0,1:T(8,128)(2,1)S(1)}, bf16[32,20,1024]{2,0,1:T(8,128)(2,1)}, u32[]{:S(2)}, u32[]{:S(2)}) %collective-permute-start.3) | collective-permute-done | bytes 1310752 | tf_op jit(solution)/shard_map/ppermute | solution.py:84
  79.9 0.3 convolution_convert_fusion.1
  80.2 0.2 broadcast_in_dim.12
  80.4 26.8 %all_to_all.21 = bf16[32,20,1024]{2,1,0:T(8,128)(2,1)S(1)} all-to-all(bf16[32,20,1024]{2,1,0:T(8,128)(2,1)S(1)} %bitcast.98), channel_id=1, replica_groups=mesh['dp'=32,'tensor'=4] {'dp'}, dimensions={0} | all-to-all | bytes 2621440 | tf_op jit(solution)/shard_map/all_to_all | solution.py:74
  107.3 1.8 copy.72
  109.1 1.3 collective-permute-start
  110.4 0.8 collective-permute-done.4
  111.2 0.2 collective-permute-start.5
  111.4 2.0 copy.83
  113.5 27.7 %collective-permute-done = bf16[32,20,1024]{2,0,1:T(8,128)(2,1)} collective-permute-done((bf16[32,20,1024]{2,0,1:T(8,128)(2,1)}, bf16[32,20,1024]{2,0,1:T(8,128)(2,1)}, u32[]{:S(2)}, u32[]{:S(2)}) %collective-permute-start) | collective-permute-done | bytes 1310752 | tf_op jit(solution)/shard_map/ppermute | solution.py:84
  141.3 2.0 copy.82
  143.3 25.9 %collective-permute-done.5 = bf16[32,20,1024]{2,0,1:T(8,128)(2,1)} collective-permute-done((bf16[32,20,1024]{2,0,1:T(8,128)(2,1)}, bf16[32,20,1024]{2,0,1:T(8,128)(2,1)}, u32[]{:S(2)}, u32[]{:S(2)}) %collective-permute-start.5) | collective-permute-done | bytes 1310752 | tf_op jit(solution)/shard_map/ppermute | solution.py:84
  169.3 2.1 copy.81
  171.3 11.9 %fusion.21 = bf16[32,20,4096]{2,1,0:T(8,128)(2,1)} fusion(s32[]{:T(128)S(6)} %select_n.23, bf16[32,20,1024]{2,1,0:T(8,128)(2,1)S(1)} %copy.81, bf16[32,20,1024]{2,1,0:T(8,128)(2,1)S(1)} %copy.82, bf16[32,20,1024]{2,1,0:T(8,128)(2,1)S(1)} %copy.83, bf16[32,20,1024]{2,1,0:T(8,128)(2,1)S(1)} %all_to_all.20), kind=kLoop, calls=%fused_computation.35 | loop fusion | flops 41943040 | bytes 10485764 | tf_op jit(solution)/shard_map/jit(_roll_dynamic)/concatenate | solution.py:86
  183.2 7.8 %reshape.140 = bf16[640,4096]{1,0:T(8,128)(2,1)} reshape(bf16[32,20,4096]{2,1,0:T(8,128)(2,1)} %fusion.21) | data formatting | bytes 10485760 | tf_op jit(solution)/shard_map/reshape | solution.py:91
  191.1 10.7 %fusion.8 = f32[640,896]{1,0:T(8,128)} fusion(bf16[640,4096]{1,0:T(8,128)(2,1)} %reshape.140, bf16[1,4096,896]{2,1,0:T(8,128)(2,1)} %param.13), kind=kOutput, calls=%fused_computation.26 | convolution fusion | flops 4697620480 | bytes 14876672 | tf_op jit(solution)/shard_map/dot_general | solution.py:92
  201.7 19.1 %fusion.15 = bf16[640,4096]{1,0:T(8,128)(2,1)} fusion(bf16[1,896,4096]{2,1,0:T(8,128)(2,1)} %param.15, f32[640,896]{1,0:T(8,128)} %fusion.8, bf16[640,4096]{1,0:T(8,128)(2,1)} %reshape.140, bf16[1,4096,896]{2,1,0:T(8,128)(2,1)} %param.14), kind=kOutput, calls=%fused_computation.31 | convolution fusion | flops 9401303040 | bytes 27459584 | tf_op jit(solution)/shard_map/dot_general | solution.py:95
  220.9 0.1 collective-permute-start.2
  221.1 2.0 copy.75
  223.1 2.1 copy.74
  225.2 48.7 %collective-permute-done.2 = bf16[32,20,1024]{2,0,1:T(8,128)(2,1)S(1)} collective-permute-done((bf16[32,20,1024]{2,0,1:T(8,128)(2,1)}, bf16[32,20,1024]{2,0,1:T(8,128)(2,1)S(1)}, u32[]{:S(2)}, u32[]{:S(2)}) %collective-permute-start.2) | collective-permute-done | bytes 1310752 | tf_op jit(solution)/shard_map/ppermute | solution.py:84
  273.9 0.7 copy.73
  274.6 12.1 %fusion.28 = bf16[32,20,4096]{2,1,0:T(8,128)(2,1)} fusion(s32[]{:T(128)S(6)} %select_n.23, bf16[32,20,1024]{2,1,0:T(8,128)(2,1)S(1)} %copy.73, bf16[32,20,1024]{2,1,0:T(8,128)(2,1)S(1)} %copy.74, bf16[32,20,1024]{2,1,0:T(8,128)(2,1)S(1)} %copy.75, bf16[32,20,1024]{2,1,0:T(8,128)(2,1)S(1)} %all_to_all.21), kind=kLoop, calls=%fused_computation.42 | loop fusion | flops 41943040 | bytes 10485764 | tf_op jit(solution)/shard_map/jit(_roll_dynamic)/concatenate | solution.py:86
  286.8 7.8 %reshape.135 = bf16[640,4096]{1,0:T(8,128)(2,1)} reshape(bf16[32,20,4096]{2,1,0:T(8,128)(2,1)} %fusion.28) | data formatting | bytes 10485760 | tf_op jit(solution)/shard_map/reshape | solution.py:91
  294.5 11.7 %fusion.10 = f32[640,896]{1,0:T(8,128)S(1)} fusion(bf16[640,4096]{1,0:T(8,128)(2,1)} %reshape.135, bf16[1,4096,896]{2,1,0:T(8,128)(2,1)} %param.13), kind=kOutput, calls=%fused_computation.28 | convolution fusion | flops 4697620480 | bytes 14876672 | tf_op jit(solution)/shard_map/dot_general | solution.py:92
  306.2 18.7 %fusion.12 = bf16[640,4096]{1,0:T(8,128)(2,1)} fusion(bf16[1,896,4096]{2,1,0:T(8,128)(2,1)} %param.15, f32[640,896]{1,0:T(8,128)S(1)} %fusion.10, bf16[640,4096]{1,0:T(8,128)(2,1)} %reshape.135, bf16[1,4096,896]{2,1,0:T(8,128)(2,1)} %param.14), kind=kOutput, calls=%fused_computation.30 | convolution fusion | flops 9401303040 | bytes 27459584 | tf_op jit(solution)/shard_map/dot_general | solution.py:95
  325.0 3.2 convert_element_type.98
  328.2 7.7 %all-to-all-start.3 = ((bf16[32,20,1024]{2,1,0:T(8,128)(2,1)}), bf16[32,20,1024]{2,1,0:T(8,128)(2,1)S(1)}, u32[]{:S(2)}, u32[]{:S(2)}) async-start(bf16[32,20,1024]{2,1,0:T(8,128)(2,1)} %convert_element_type.98), calls=%async_computation.5 | async-start | bytes 3145728 | tf_op jit(solution)/shard_map/all_to_all | solution.py:99
  336.0 41.4 %reduce-scatter.3.cloned.1.call-done = bf16[640,1024]{1,0:T(8,128)(2,1)} async-done(((bf16[640,4096]{1,0:T(8,128)(2,1)}), bf16[640,1024]{1,0:T(8,128)(2,1)}) %reduce-scatter.3.cloned.1.call-update) | async-done | bytes 1310736 | tf_op jit(solution)/shard_map/reduce_scatter | solution.py:96
  377.4 3.2 convert_element_type.90
  380.6 7.7 %all-to-all-start.1 = ((bf16[32,20,1024]{2,1,0:T(8,128)(2,1)}), bf16[32,20,1024]{2,1,0:T(8,128)(2,1)S(1)}, u32[]{:S(2)}, u32[]{:S(2)}) async-start(bf16[32,20,1024]{2,1,0:T(8,128)(2,1)} %convert_element_type.90), calls=%async_computation.2 | async-start | bytes 3145728 | tf_op jit(solution)/shard_map/all_to_all | solution.py:99
  388.6 76.7 %psum.7 = f32[32]{0:T(128)S(1)} all-reduce(f32[32]{0:T(128)S(1)} %pad_maximum_fusion.4), channel_id=1, replica_groups=mesh['dp'=32,'tensor'=4] {'dp'}, use_global_device_ids=true, to_apply=%region_18.21 | all-reduce | flops 32 | bytes 256 | tf_op jit(solution)/shard_map/psum | solution.py:12
  465.4 0.6 pad_maximum_fusion.3
  466.0 1.2 convert_reduce_fusion
  467.1 1.2 reshape.143
  468.4 0.3 convert_reduce_fusion.1
  468.7 0.5 fusion.43
  469.2 0.5 fusion.42
  469.7 0.7 pad_maximum_fusion
  (36 shorter events, 1.5 us)
Async XLA Ops:
  7.2 317.8 %reduce-scatter.5.cloned.1.call-start = ((), (), s32[]{:S(2)}) async-start(), calls=%async_computation.7 | async-start | bytes 6553600 | tf_op jit(solution)/shard_map/reduce_scatter | solution.py:96
  13.0 1.3 copy-start.1
  13.0 1.5 copy-start
  47.8 32.1 %collective-permute-start.3 = (bf16[32,20,1024]{2,0,1:T(8,128)(2,1)S(1)}, bf16[32,20,1024]{2,0,1:T(8,128)(2,1)}, u32[]{:S(2)}, u32[]{:S(2)}) collective-permute-start(bf16[32,20,1024]{2,0,1:T(8,128)(2,1)S(1)} %copy.80), channel_id=1, source_target_pairs={{0,1},{1,2},{2,3},{3,0},{4,5},{5,6},{6,7},{7,4},{8,9},{9,10},{10,1... | collective-permute-start | bytes 3932168 | tf_op jit(solution)/shard_map/ppermute | solution.py:84
  79.9 31.3 %collective-permute-start.4 = (bf16[32,20,1024]{2,0,1:T(8,128)(2,1)}, bf16[32,20,1024]{2,0,1:T(8,128)(2,1)}, u32[]{:S(2)}, u32[]{:S(2)}) collective-permute-start(bf16[32,20,1024]{2,0,1:T(8,128)(2,1)} %collective-permute-done.3), channel_id=1, source_target_pairs={{0,1},{1,2},{2,3},{3,0},{4,5},{5,6},{6,7},{7,4},{8,9},{9,10},{10,1... | collective-permute-start | bytes 3932168 | tf_op jit(solution)/shard_map/ppermute | solution.py:84
  109.1 32.1 %collective-permute-start = (bf16[32,20,1024]{2,0,1:T(8,128)(2,1)}, bf16[32,20,1024]{2,0,1:T(8,128)(2,1)}, u32[]{:S(2)}, u32[]{:S(2)}) collective-permute-start(bf16[32,20,1024]{2,0,1:T(8,128)(2,1)} %copy.72), channel_id=1, source_target_pairs={{0,1},{1,2},{2,3},{3,0},{4,5},{5,6},{6,7},{7,4},{8,9},{9,10},{10,1... | collective-permute-start | bytes 3932168 | tf_op jit(solution)/shard_map/ppermute | solution.py:84
  111.2 58.1 %collective-permute-start.5 = (bf16[32,20,1024]{2,0,1:T(8,128)(2,1)}, bf16[32,20,1024]{2,0,1:T(8,128)(2,1)}, u32[]{:S(2)}, u32[]{:S(2)}) collective-permute-start(bf16[32,20,1024]{2,0,1:T(8,128)(2,1)} %collective-permute-done.4), channel_id=1, source_target_pairs={{0,1},{1,2},{2,3},{3,0},{4,5},{5,6},{6,7},{7,4},{8,9},{9,10},{10,1... | collective-permute-start | bytes 3932168 | tf_op jit(solution)/shard_map/ppermute | solution.py:84
  141.2 79.7 %collective-permute-start.1 = (bf16[32,20,1024]{2,0,1:T(8,128)(2,1)}, bf16[32,20,1024]{2,0,1:T(8,128)(2,1)}, u32[]{:S(2)}, u32[]{:S(2)}) collective-permute-start(bf16[32,20,1024]{2,0,1:T(8,128)(2,1)} %collective-permute-done), channel_id=1, source_target_pairs={{0,1},{1,2},{2,3},{3,0},{4,5},{5,6},{6,7},{7,4},{8,9},{9,10},{10,1... | collective-permute-start | bytes 3932168 | tf_op jit(solution)/shard_map/ppermute | solution.py:84
  220.9 156.5 %reduce-scatter.3.cloned.1.call-start = ((), (), s32[]{:S(2)}) async-start(), calls=%async_computation.6 | async-start | bytes 6553600 | tf_op jit(solution)/shard_map/reduce_scatter | solution.py:96
  220.9 52.9 %collective-permute-start.2 = (bf16[32,20,1024]{2,0,1:T(8,128)(2,1)}, bf16[32,20,1024]{2,0,1:T(8,128)(2,1)S(1)}, u32[]{:S(2)}, u32[]{:S(2)}) collective-permute-start(bf16[32,20,1024]{2,0,1:T(8,128)(2,1)} %collective-permute-done.1), channel_id=1, source_target_pairs={{0,1},{1,2},{2,3},{3,0},{4,5},{5,6},{6,7},{7,4},{8,9},{9,10},{10,1... | collective-permute-start | bytes 3932168 | tf_op jit(solution)/shard_map/ppermute | solution.py:84
  328.2 52.4 %all-to-all-start.3 = ((bf16[32,20,1024]{2,1,0:T(8,128)(2,1)}), bf16[32,20,1024]{2,1,0:T(8,128)(2,1)S(1)}, u32[]{:S(2)}, u32[]{:S(2)}) async-start(bf16[32,20,1024]{2,1,0:T(8,128)(2,1)} %convert_element_type.98), calls=%async_computation.5 | async-start | bytes 3145728 | tf_op jit(solution)/shard_map/all_to_all | solution.py:99
  380.6 87.8 %all-to-all-start.1 = ((bf16[32,20,1024]{2,1,0:T(8,128)(2,1)}), bf16[32,20,1024]{2,1,0:T(8,128)(2,1)S(1)}, u32[]{:S(2)}, u32[]{:S(2)}) async-start(bf16[32,20,1024]{2,1,0:T(8,128)(2,1)} %convert_element_type.90), calls=%async_computation.2 | async-start | bytes 3145728 | tf_op jit(solution)/shard_map/all_to_all | solution.py:99
Sparse Core Ops, SparseCore 0:
  221.0 75.8 reduce-scatter.4
  325.1 52.2 reduce-scatter.2
